TPU v7x, 32 devices: a whole 2x2x4 slice. The times are simulated.
32 devices in a mesh: grp: 1, mid: 16 (over z, y, core), off: 2 (over x), sub: 1.
Axes of the slice: x: 2, y: 2, z: 4, core: 2. Of those that a mesh axis runs over, the one named last changes fastest.
Arguments:
- traces: bfloat16 [2, 1024, 1024], P('off', ('grp', 'mid'), 'sub'), may hold values from -6 to 6
- centre_offset: int32 [256], P(('grp', 'mid')), may hold values from 0 to 63
- foot_start: int32 [256, 16], P('grp'), may hold values from 0 to 240
- beam_count: int32 [16], P('grp'), may hold values from 2 to 16, as said below
- operator: bfloat16 [1024, 65536], P('sub', 'mid'), may hold values from -0.1875 to 0.1875
Outputs:
- image: float32 [256, 256], P(('grp', 'mid'))
Inputs may be any that keep to these rules, and one draw needn't show every extreme that they name: `beam_count`: the live beams of all tiles sum to exactly 128, and the largest count is exactly 16.
All inputs are finite; a program needn't handle non-finite values.
Results may differ from a plain program's by a relative error of at most 0.0028.
Values may be sent and summed in bfloat16 or wider, within the bound.
No kernel may reach another device: no remote copies, remote signals or barrier semaphores. Data moves between devices by JAX's collectives and lax.ppermute only.
A program may use at most 64 MiB of HBM per device.

v0:
```python
import math
import jax
import jax.numpy as jnp
from jax import lax
from jax.sharding import PartitionSpec as P

NT = 1024
P_SIZE = 16
FL = 16
DEPTH = 256
HALF = 16
CB_DEV = 16


def padded_2(cells, sides, width):
    for axis, dim in sides:
        count = lax.axis_size(axis)
        ends = count - 1
        head = lax.slice_in_dim(cells, 0, width, axis=dim)
        tail = lax.slice_in_dim(cells, cells.shape[dim] - width, cells.shape[dim], axis=dim)
        cells = jnp.concatenate(
            [
                lax.ppermute(tail, axis, [(i, (i + 1) % count) for i in range(ends)]),
                cells,
                lax.ppermute(head, axis, [((i + 1) % count, i) for i in range(ends)]),
            ],
            axis=dim,
        )
    return cells


def dft_rows(first_row, row_count, freq_block):
    sample_index = first_row + jnp.arange(row_count, dtype=jnp.int32)[:, None]
    column = jnp.arange(NT, dtype=jnp.int32)[None, :]
    within = column % (2 * freq_block)
    frequency = column // (2 * freq_block) * freq_block + within % freq_block
    phase_angle = 2.0 * math.pi / NT * (sample_index * frequency % NT).astype(jnp.float32)
    values = jnp.where(within // freq_block == 1, -jnp.sin(phase_angle), jnp.cos(phase_angle))
    return values / math.sqrt(NT)


def slant_weights(frequency):
    offsets = jnp.arange(-HALF, HALF + 1, dtype=jnp.int32).astype(jnp.float32)
    taper = jnp.exp(-0.5 * (1.5 * offsets / HALF) ** 2)
    taper = taper / jnp.sqrt(jnp.sum(taper * taper))
    slopes = 0.25 * (jnp.arange(P_SIZE, dtype=jnp.int32).astype(jnp.float32) - 0.5 * (P_SIZE - 1))
    theta = (
        2.0
        * math.pi
        / NT
        * slopes[:, None, None]
        * offsets[None, :, None]
        * frequency.astype(jnp.float32)[None, None, :]
    )
    return (taper[None, :, None] * jnp.cos(theta), taper[None, :, None] * jnp.sin(theta))


def form_beams(windows_real, windows_imag, cos_weight, sin_weight):
    high = lax.Precision.HIGHEST
    beam_real = jnp.einsum("pxf,bxf->bpf", cos_weight, windows_real, precision=high) + jnp.einsum(
        "pxf,bxf->bpf", sin_weight, windows_imag, precision=high
    )
    beam_imag = jnp.einsum("pxf,bxf->bpf", cos_weight, windows_imag, precision=high) - jnp.einsum(
        "pxf,bxf->bpf", sin_weight, windows_real, precision=high
    )
    return (beam_real, beam_imag)


def live_rows(beam_count, per_tile, live_total):
    tile_ends = jnp.cumsum(beam_count)
    position = jnp.arange(live_total, dtype=jnp.int32)
    owner = jnp.sum((position[:, None] >= tile_ends[None, :]).astype(jnp.int32), axis=1)
    first = tile_ends - beam_count
    match = owner[:, None] == jnp.arange(beam_count.shape[0], dtype=jnp.int32)[None, :]
    chosen = jnp.sum(jnp.where(match, first[None, :], 0), axis=1)
    return owner * per_tile + position - chosen


def spread_slopes(beams, mid_count):
    return jnp.repeat(beams, mid_count // P_SIZE, axis=1)[:, :, None, :]


def shards(traces, centre_offset, foot_start, beam_count, operator):
    high = lax.Precision.HIGHEST
    mid_count = lax.axis_size("mid")
    mid_index = lax.axis_index("mid")
    sub_index = lax.axis_index("sub")
    samples = traces.shape[2]
    freq_block = samples // 2
    dft_table = dft_rows(sub_index * samples, samples, freq_block)
    partial_value = jnp.dot(traces[0].astype(jnp.float32), dft_table, precision=high)
    spectrum = lax.psum_scatter(partial_value, "sub", scatter_dimension=1, tiled=True)
    padded = padded_2(spectrum, (("mid", 0),), HALF)
    window_index = centre_offset[:, None] + jnp.arange(2 * HALF + 1, dtype=jnp.int32)[None, :]
    windows = padded[window_index]
    frequency = sub_index * freq_block + jnp.arange(freq_block, dtype=jnp.int32)
    cos_weight, sin_weight = slant_weights(frequency)
    beam_real, beam_imag = form_beams(
        windows[:, :, :freq_block], windows[:, :, freq_block:], cos_weight, sin_weight
    )
    live_here = lax.dynamic_index_in_dim(beam_count, mid_index, 0, keepdims=False)
    alive = jnp.arange(CB_DEV, dtype=jnp.int32) < live_here
    beams = jnp.where(
        alive[:, None, None], jnp.concatenate([beam_real, beam_imag], axis=2), 0.0
    ).astype(jnp.bfloat16)
    columns = operator.shape[1]
    slope_count = max(1, P_SIZE // mid_count)
    footprint_size = FL * DEPTH
    first_column = mid_index * columns
    slope_first = first_column // footprint_size
    lateral_first = first_column % footprint_size // DEPTH
    lateral_count = columns // (slope_count * DEPTH)
    starts = lax.dynamic_slice_in_dim(foot_start, slope_first, slope_count, 1)
    kernels = operator.reshape(samples, slope_count, lateral_count * DEPTH)
    outgoing = spread_slopes(beams, mid_count)
    received = lax.all_to_all(outgoing, "mid", split_axis=1, concat_axis=0, tiled=True)
    row_total = received.shape[0]
    received = received.reshape(row_total, slope_count, samples)
    chosen = live_rows(beam_count, CB_DEV, row_total // 2)
    received = received[chosen]
    starts = starts[chosen]
    centres_all = CB_DEV * mid_count
    block_rows = received.shape[0] // 8
    lateral_steps = lateral_first + jnp.arange(lateral_count, dtype=jnp.int32)
    weight_scale = 1.0 / math.sqrt(FL * P_SIZE)

    def add_block(block, partial_image):
        block_beams = lax.dynamic_slice_in_dim(received, block * block_rows, block_rows, 0)
        block_starts = lax.dynamic_slice_in_dim(starts, block * block_rows, block_rows, 0)
        footprint = (
            jnp.einsum(
                "rsk,ksc->rsc",
                block_beams,
                kernels,
                preferred_element_type=jnp.float32,
                precision=None,
            )
            * weight_scale
        )
        target = (block_starts[:, :, None] + lateral_steps[None, None, :]).reshape(-1)
        return partial_image.at[target].add(footprint.reshape(-1, DEPTH))

    partial_image = lax.fori_loop(0, 8, add_block, jnp.zeros((centres_all, DEPTH), jnp.float32))
    tile_part = lax.psum_scatter(partial_image, "mid", scatter_dimension=0, tiled=True)
    image_tile = lax.psum(tile_part, ("off", "sub"))
    return image_tile


def solution(mesh):
    return jax.shard_map(
        shards,
        mesh=mesh,
        in_specs=(
            P("off", ("grp", "mid"), "sub"),
            P(("grp", "mid")),
            P("grp", None),
            P("grp"),
            P("sub", "mid"),
        ),
        out_specs=P(("grp", "mid"), None),
        check_vma=False,
    )
```

profile of v0, /device:TPU:0, one launch (start us, length us, event | category | flops | bytes accessed | tf_op | source)
XLA Modules:
  0.0 302.9 jit_solution(10258780660640773657)
XLA Ops:
  6.6 0.9 copy-done
  7.4 19.2 %fusion.60 = f32[64,1024]{1,0:T(8,128)S(1)} fusion(s32[1024]{0:T(1024)S(1)} %fusion.67, pred[1024]{0:T(1024)(128)(4,1)S(1)} %fusion.64, bf16[1,64,1024]{2,1,0:T(8,128)(2,1)S(1)} %copy-done), kind=kOutput, calls=%fused_computation.61 | convolution fusion | flops 823132160 | bytes 398336 | tf_op jit(solution)/shard_map/dot_general | solution.py:91
  26.7 2.4 collective-permute-start
  29.1 1.5 collective-permute-start.1
  30.6 0.6 multiply_reduce_fusion
  32.2 0.6 dynamic_slice.24
  32.8 0.6 iota_compare_fusion.2
  33.4 0.9 collective-permute-done.1
  34.4 2.5 gather_fusion.1
  36.8 1.7 reshape.394
  38.5 2.0 fusion.81
  40.5 3.7 %copy.23 = f32[16,33,512]{1,0,2:T(8,128)} copy(f32[16,33,512]{2,1,0:T(8,128)S(1)} %get-tuple-element.148) | data formatting | bytes 2162688
  44.2 3.8 %copy.24 = f32[16,33,512]{1,0,2:T(8,128)} copy(f32[16,33,512]{2,1,0:T(8,128)S(1)} %get-tuple-element.149) | data formatting | bytes 2162688
  48.0 24.9 %fusion.16 = f32[512,16,16]{2,1,0:T(8,128)S(1)} fusion(f32[16,33,512]{1,0,2:T(8,128)} %copy.23, f32[512]{0:T(512)S(1)} %iota_convert_fusion, f32[16,33]{1,0:T(8,128)S(1)} %broadcast_multiply_fusion, f32[33]{0:T(128)S(1)} %broadcast_divide_fusion), kind=kOutput, calls=%fused_computation.24 | convolution fusion | flops 52445184 | bytes 1609924 | tf_op jit(solution)/shard_map/pxf,bxf->bpf/dot_general | solution.py:60
  72.9 22.2 %fusion.14 = f32[512,16,16]{2,1,0:T(8,128)S(1)} fusion(f32[16,33,512]{1,0,2:T(8,128)S(1)} %copy-done.3, f32[512]{0:T(512)S(1)} %iota_convert_fusion, f32[16,33]{1,0:T(8,128)S(1)} %broadcast_multiply_fusion, f32[33]{0:T(128)S(1)} %broadcast_divide_fusion), kind=kOutput, calls=%fused_computation.23 | convolution fusion | flops 52445184 | bytes 1609924 | tf_op jit(solution)/shard_map/pxf,bxf->bpf/dot_general | solution.py:63
  95.1 23.7 %add_bitcast_fusion = bf16[16,16,1,512]{1,0,3,2:T(8,128)(2,1)S(1)} fusion(f32[512,16,16]{2,1,0:T(8,128)S(1)} %fusion.16, f32[16,33,512]{1,0,2:T(8,128)S(1)} %copy-done.3, f32[512]{0:T(512)S(1)} %iota_convert_fusion, f32[16,33]{1,0:T(8,128)S(1)} %broadcast_multiply_fusion, f32[33]{0:T(128)S(1)} %broadcast_divide_fusion), kind=kOutput, calls=%fused_computation.32 | convolution fusion | flops 52707328 | bytes 1872068 | tf_op jit(solution)/shard_map/pxf,bxf->bpf/dot_general | solution.py:60
  118.9 23.7 %subtract_bitcast_fusion = bf16[16,16,1,512]{1,0,3,2:T(8,128)(2,1)S(1)} fusion(f32[512,16,16]{2,1,0:T(8,128)S(1)} %fusion.14, f32[16,33,512]{1,0,2:T(8,128)S(1)} %copy-done.2, f32[512]{0:T(512)S(1)} %iota_convert_fusion, f32[16,33]{1,0:T(8,128)S(1)} %broadcast_multiply_fusion, f32[33]{0:T(128)S(1)} %broadcast_divide_fusion), kind=kOutput, calls=%fused_computation.31 | convolution fusion | flops 52707328 | bytes 1872068 | tf_op jit(solution)/shard_map/pxf,bxf->bpf/dot_general | solution.py:63
  142.6 2.6 maximum_select_fusion
  145.2 5.7 %copy.22 = bf16[16,16,1,1024]{3,0,2,1:T(8,128)(2,1)} copy(bf16[16,16,1,1024]{1,0,3,2:T(8,128)(2,1)} %maximum_select_fusion) | data formatting | bytes 1048576 | tf_op jit(solution)/shard_map/jit(_where)/select_n | solution.py:103
  150.8 8.4 %all-to-all-start = ((bf16[16,16,1,1024]{3,0,2,1:T(8,128)(2,1)}), bf16[16,16,1,1024]{3,0,2,1:T(8,128)(2,1)S(1)}, u32[]{:S(2)}, u32[]{:S(2)}) async-start(bf16[16,16,1,1024]{3,0,2,1:T(8,128)(2,1)} %copy.22), calls=%async_computation | async-start | bytes 1048576 | tf_op jit(solution)/shard_map/all_to_all | solution.py:116
  159.2 0.3 reduce-scatter.2.cloned.1.call-start
  159.7 0.1 reduce.1
  159.8 0.7 constant_dynamic-slice_fusion
  160.7 1.3 gather_fusion
  162.0 11.5 %all-to-all-done = bf16[16,16,1,1024]{3,0,2,1:T(8,128)(2,1)S(1)} async-done(((bf16[16,16,1,1024]{3,0,2,1:T(8,128)(2,1)}), bf16[16,16,1,1024]{3,0,2,1:T(8,128)(2,1)S(1)}, u32[]{:S(2)}, u32[]{:S(2)}) %all-to-all-start) | async-done | bytes 524320 | tf_op jit(solution)/shard_map/all_to_all | solution.py:116
  173.5 0.9 gather_fusion.2
  174.4 56.2 %while.14 = (s32[]{:T(128)}, f32[256,256]{1,0:T(8,128)S(1)}, s32[128,1]{0,1:T(1,128)S(1)}, bf16[128,1,1024]{2,0,1:T(8,128)(2,1)S(1)}, bf16[1024,1,4096]{2,0,1:T(...) while((s32[]{:T(128)}, f32[256,256]{1,0:T(8,128)S(1)}, ...), condition=%wide.region_6.7_spmd.clone, body=%wide.region_4.6_spmd.clone.sunk | while | flops 134349840 | bytes 10000863 | solution.py:143
  174.4 4.6 %fusion.92 = f32[16,1,4096]{2,0,1:T(8,128)S(1)} fusion(bf16[1024,1,4096]{2,0,1:T(8,128)(2,1)} %get-tuple-element.213, bf16[128,1,1024]{2,0,1:T(8,128)(2,1)S(1)} %get-tuple-element.212, s32[]{:T(128)S(6)} %select_n.211), kind=kOutput, calls=%fused_computation.8.clone.1 | convolution fusion | flops 134283264 | bytes 8683524 | tf_op jit(solution)/shard_map/while/body/eval_jaxpr/rsk,ksc->rsc/dot_general | solution.py:131
  179.1 0.1 add_reduce_fusion.2
  179.3 2.1 scatter_fusion
  181.4 4.6 %fusion.92 = f32[16,1,4096]{2,0,1:T(8,128)S(1)} fusion(bf16[1024,1,4096]{2,0,1:T(8,128)(2,1)} %get-tuple-element.213, bf16[128,1,1024]{2,0,1:T(8,128)(2,1)S(1)} %get-tuple-element.212, s32[]{:T(128)S(6)} %select_n.211), kind=kOutput, calls=%fused_computation.8.clone.1 | convolution fusion | flops 134283264 | bytes 8683524 | tf_op jit(solution)/shard_map/while/body/eval_jaxpr/rsk,ksc->rsc/dot_general | solution.py:131
  186.1 0.1 add_reduce_fusion.2
  186.3 2.1 scatter_fusion
  188.4 4.6 %fusion.92 = f32[16,1,4096]{2,0,1:T(8,128)S(1)} fusion(bf16[1024,1,4096]{2,0,1:T(8,128)(2,1)} %get-tuple-element.213, bf16[128,1,1024]{2,0,1:T(8,128)(2,1)S(1)} %get-tuple-element.212, s32[]{:T(128)S(6)} %select_n.211), kind=kOutput, calls=%fused_computation.8.clone.1 | convolution fusion | flops 134283264 | bytes 8683524 | tf_op jit(solution)/shard_map/while/body/eval_jaxpr/rsk,ksc->rsc/dot_general | solution.py:131
  193.3 2.1 scatter_fusion
  195.5 4.6 %fusion.92 = f32[16,1,4096]{2,0,1:T(8,128)S(1)} fusion(bf16[1024,1,4096]{2,0,1:T(8,128)(2,1)} %get-tuple-element.213, bf16[128,1,1024]{2,0,1:T(8,128)(2,1)S(1)} %get-tuple-element.212, s32[]{:T(128)S(6)} %select_n.211), kind=kOutput, calls=%fused_computation.8.clone.1 | convolution fusion | flops 134283264 | bytes 8683524 | tf_op jit(solution)/shard_map/while/body/eval_jaxpr/rsk,ksc->rsc/dot_general | solution.py:131
  200.4 2.1 scatter_fusion
  202.5 4.6 %fusion.92 = f32[16,1,4096]{2,0,1:T(8,128)S(1)} fusion(bf16[1024,1,4096]{2,0,1:T(8,128)(2,1)} %get-tuple-element.213, bf16[128,1,1024]{2,0,1:T(8,128)(2,1)S(1)} %get-tuple-element.212, s32[]{:T(128)S(6)} %select_n.211), kind=kOutput, calls=%fused_computation.8.clone.1 | convolution fusion | flops 134283264 | bytes 8683524 | tf_op jit(solution)/shard_map/while/body/eval_jaxpr/rsk,ksc->rsc/dot_general | solution.py:131
  207.4 2.1 scatter_fusion
  209.5 4.6 %fusion.92 = f32[16,1,4096]{2,0,1:T(8,128)S(1)} fusion(bf16[1024,1,4096]{2,0,1:T(8,128)(2,1)} %get-tuple-element.213, bf16[128,1,1024]{2,0,1:T(8,128)(2,1)S(1)} %get-tuple-element.212, s32[]{:T(128)S(6)} %select_n.211), kind=kOutput, calls=%fused_computation.8.clone.1 | convolution fusion | flops 134283264 | bytes 8683524 | tf_op jit(solution)/shard_map/while/body/eval_jaxpr/rsk,ksc->rsc/dot_general | solution.py:131
  214.4 2.1 scatter_fusion
  216.5 4.6 %fusion.92 = f32[16,1,4096]{2,0,1:T(8,128)S(1)} fusion(bf16[1024,1,4096]{2,0,1:T(8,128)(2,1)} %get-tuple-element.213, bf16[128,1,1024]{2,0,1:T(8,128)(2,1)S(1)} %get-tuple-element.212, s32[]{:T(128)S(6)} %select_n.211), kind=kOutput, calls=%fused_computation.8.clone.1 | convolution fusion | flops 134283264 | bytes 8683524 | tf_op jit(solution)/shard_map/while/body/eval_jaxpr/rsk,ksc->rsc/dot_general | solution.py:131
  221.4 2.1 scatter_fusion
  223.5 4.6 %fusion.92 = f32[16,1,4096]{2,0,1:T(8,128)S(1)} fusion(bf16[1024,1,4096]{2,0,1:T(8,128)(2,1)} %get-tuple-element.213, bf16[128,1,1024]{2,0,1:T(8,128)(2,1)S(1)} %get-tuple-element.212, s32[]{:T(128)S(6)} %select_n.211), kind=kOutput, calls=%fused_computation.8.clone.1 | convolution fusion | flops 134283264 | bytes 8683524 | tf_op jit(solution)/shard_map/while/body/eval_jaxpr/rsk,ksc->rsc/dot_general | solution.py:131
  228.4 2.1 scatter_fusion
  230.5 0.7 copy-done.1
  231.3 55.4 %reduce-scatter.2.cloned.1.call-done = f32[16,256]{1,0:T(8,128)} async-done(((f32[256,256]{1,0:T(8,128)}), f32[16,256]{1,0:T(8,128)}) %reduce-scatter.2.cloned.1.call-update) | async-done | bytes 16400 | tf_op jit(solution)/shard_map/reduce_scatter | solution.py:144
  286.7 9.4 %psum.7 = f32[16,256]{1,0:T(8,128)} all-reduce(f32[16,256]{1,0:T(8,128)} %reduce-scatter.2.cloned.1.call-done), channel_id=1, replica_groups=mesh['grp'=1,'mid'=16,'off'=2,'sub'=1] {'off','sub'}, use_global_device_ids=true, to_apply=%region_8.9 | all-reduce | flops 4096 | bytes 32768 | tf_op jit(solution)/shard_map/psum | solution.py:145
  (78 shorter events, 3.0 us)
Async XLA Ops:
  6.5 0.9 copy-start
  7.4 23.8 %copy-start.4 = (s32[16]{0:T(128)S(1)}, s32[16]{0:T(128)}, u32[]{:S(2)}) copy-start(s32[16]{0:T(128)} %param.8) | copy-start | bytes 196
  7.4 24.7 %copy-start.5 = (s32[16]{0:T(128)S(1)}, s32[16]{0:T(128)}, u32[]{:S(2)}) copy-start(s32[16]{0:T(128)} %param.10) | copy-start | bytes 196
  26.7 6.7 %collective-permute-start = (f32[16,1024]{1,0:T(8,128)S(1)}, f32[16,1024]{1,0:T(8,128)S(1)}, u32[]{:S(2)}, u32[]{:S(2)}) collective-permute-start(f32[16,1024]{1,0:T(8,128)S(1)} %get-tuple-element.150), channel_id=1, source_target_pairs={{0,2},{2,4},{4,6},{6,8},{8,10},{10,12},{12,14},{14,16},{16,18},{18... | collective-permute-start | bytes 196616 | tf_op jit(solution)/shard_map/ppermute | solution.py:23
  29.1 5.3 %collective-permute-start.1 = (f32[16,1024]{1,0:T(8,128)S(1)}, f32[16,1024]{1,0:T(8,128)S(1)}, u32[]{:S(2)}, u32[]{:S(2)}) collective-permute-start(f32[16,1024]{1,0:T(8,128)S(1)} %get-tuple-element.151), channel_id=1, source_target_pairs={{2,0},{4,2},{6,4},{8,6},{10,8},{12,10},{14,12},{16,14},{18,16},{20... | collective-permute-start | bytes 196616 | tf_op jit(solution)/shard_map/ppermute | solution.py:25
  48.0 24.9 %copy-start.3 = (f32[16,33,512]{1,0,2:T(8,128)S(1)}, f32[16,33,512]{1,0,2:T(8,128)}, u32[]{:S(2)}) copy-start(f32[16,33,512]{1,0,2:T(8,128)} %copy.24) | copy-start | bytes 3244036
  95.1 23.8 %copy-start.2 = (f32[16,33,512]{1,0,2:T(8,128)S(1)}, f32[16,33,512]{1,0,2:T(8,128)}, u32[]{:S(2)}) copy-start(f32[16,33,512]{1,0,2:T(8,128)} %copy.23) | copy-start | bytes 3244036
  150.8 22.7 %all-to-all-start = ((bf16[16,16,1,1024]{3,0,2,1:T(8,128)(2,1)}), bf16[16,16,1,1024]{3,0,2,1:T(8,128)(2,1)S(1)}, u32[]{:S(2)}, u32[]{:S(2)}) async-start(bf16[16,16,1,1024]{3,0,2,1:T(8,128)(2,1)} %copy.22), calls=%async_computation | async-start | bytes 1048576 | tf_op jit(solution)/shard_map/all_to_all | solution.py:116
  159.2 127.5 %reduce-scatter.2.cloned.1.call-start = ((), (), s32[]{:S(2)}) async-start(), calls=%async_computation.2 | async-start | bytes 278528 | tf_op jit(solution)/shard_map/reduce_scatter | solution.py:144
  230.5 0.7 copy-start.1
Sparse Core Ops, SparseCore 0:
  231.4 55.2 reduce-scatter.1
where the time goes:
time: 304 us; the launch traced here: 303 us
  matrix products  150 us (49%)
  waiting for transfers between devices  67.9 us (22%)
  local copies, waits for them, and re-layouts  26.1 us (9%)
  other arithmetic  21.8 us (7%)
  between operations  14.4 us (5%)
  starting transfers between devices  12.5 us (4%)
  blocking collectives  9.37 us (3%)
    reduce_scatter x1, waiting for transfers between devices, shards(): lax.psum_scatter(partial_image, 'mid', scatter_dimension=0, tiled=True)  55.4 us
    dot_general x8, matrix products, add_block(): jnp.einsum('rsk,ksc->rsc', block_beams, kernels, preferred_element_type=j...  36.7 us
    dot_general x1, matrix products, form_beams(): jnp.einsum('pxf,bxf->bpf', cos_weight, windows_real, precision=high)  24.9 us
    dot_general x1, matrix products, form_beams(): jnp.einsum('pxf,bxf->bpf', sin_weight, windows_imag, precision=high)  23.7 us
    dot_general x1, matrix products, form_beams(): jnp.einsum('pxf,bxf->bpf', sin_weight, windows_real, precision=high)  23.7 us
    dot_general x1, matrix products, form_beams(): jnp.einsum('pxf,bxf->bpf', cos_weight, windows_imag, precision=high)  22.2 us
    dot_general x1, matrix products, shards(): jnp.dot(traces[0].astype(jnp.float32), dft_table, precision=high)  19.2 us
    scatter-add x8, other arithmetic, add_block(): return partial_image.at[target].add(footprint.reshape(-1, DEPTH))  16.6 us
  transfers between devices with their start and end apart: 4, of which 3 were waited for; matrix products, arithmetic and copies ran while one was open for 1% of the time, Pallas kernels for 0%

commit v1 on v0

--- a/solution.py
+++ b/solution.py
@@ -10,6 +10,18 @@
 DEPTH = 256
 HALF = 16
 CB_DEV = 16
+
+
+def rotated_exchange(x, axis, split, join):
+    ways, here = (lax.axis_size(axis), lax.axis_index(axis))
+    width = x.shape[split] // ways
+    turned = jnp.roll(x, -here * width, axis=split)
+    got = [lax.slice_in_dim(turned, 0, width, axis=split)]
+    for far in range(1, ways):
+        sent = lax.slice_in_dim(turned, far * width, (far + 1) * width, axis=split)
+        got.append(lax.ppermute(sent, axis, [(d, (d + far) % ways) for d in range(ways)]))
+    line = jnp.concatenate(got[::-1], axis=join)
+    return jnp.roll(line, (here + 1) * got[0].shape[join], axis=join)
 
 
 def padded_2(cells, sides, width):
@@ -113,7 +125,7 @@
     starts = lax.dynamic_slice_in_dim(foot_start, slope_first, slope_count, 1)
     kernels = operator.reshape(samples, slope_count, lateral_count * DEPTH)
     outgoing = spread_slopes(beams, mid_count)
-    received = lax.all_to_all(outgoing, "mid", split_axis=1, concat_axis=0, tiled=True)
+    received = rotated_exchange(outgoing, "mid", 1, 0)
     row_total = received.shape[0]
     received = received.reshape(row_total, slope_count, samples)
     chosen = live_rows(beam_count, CB_DEV, row_total // 2)

time: 304 us -> 311 us (1.023)
  starting transfers between devices: 12.5 us -> 28.4 us
  waiting for transfers between devices: 67.9 us -> 59.6 us
    ppermute x0 -> x15, starting transfers between devices: none -> 24.5 us  [rotated_exchange(): lax.ppermute(sent, axis, [(d, (d + far) % ways) for d in range(ways)])]
    all_to_all x1 -> x0, waiting for transfers between devices: 11.5 us -> none  [shards(): lax.all_to_all(outgoing, 'mid', split_axis=1, concat_axis=0, tiled=True)]
    all_to_all x1 -> x0, starting transfers between devices: 8.38 us -> none  [shards(): lax.all_to_all(outgoing, 'mid', split_axis=1, concat_axis=0, tiled=True)]
    ppermute x0 -> x15, waiting for transfers between devices: none -> 6.01 us  [rotated_exchange(): lax.ppermute(sent, axis, [(d, (d + far) % ways) for d in range(ways)])]
    select_n x1 -> x0, local copies, waits for them, and re-layouts: 5.67 us -> none  [shards(): jnp.where(alive[:, None, None], jnp.concatenate([beam_real, beam_imag], a...]
    concatenate x0 -> x3, local copies, waits for them, and re-layouts: none -> 3.47 us  [the longest x2 3.46 us: shards(): jnp.concatenate([beam_real, beam_imag], axis=2)]
    unnamed x14 -> x58, local copies, waits for them, and re-layouts: 9.09 us -> 9.45 us
  transfers between devices with their start and end apart: 4 -> 18, of which waited for: 3 -> 6; matrix products, arithmetic and copies ran while one was open for 1% -> 2% of each run, Pallas kernels for 0% -> 0%
where the time goes in v1:
time: 311 us; the launch traced here: 310 us
  matrix products  152 us (49%)
  waiting for transfers between devices  59.6 us (19%)
  starting transfers between devices  28.4 us (9%)
  local copies, waits for them, and re-layouts  25.4 us (8%)
  other arithmetic  19.8 us (6%)
  between operations  14.6 us (5%)
  blocking collectives  9.37 us (3%)
    reduce_scatter x1, waiting for transfers between devices, shards(): lax.psum_scatter(partial_image, 'mid', scatter_dimension=0, tiled=True)  53.1 us
    dot_general x8, matrix products, add_block(): jnp.einsum('rsk,ksc->rsc', block_beams, kernels, preferred_element_type=j...  36.7 us
    dot_general x1, matrix products, form_beams(): jnp.einsum('pxf,bxf->bpf', cos_weight, windows_real, precision=high)  24.9 us
    ppermute x15, starting transfers between devices, rotated_exchange(): lax.ppermute(sent, axis, [(d, (d + far) % ways) for d in range(ways)])  24.5 us
    dot_general x1, matrix products, form_beams(): jnp.einsum('pxf,bxf->bpf', cos_weight, windows_imag, precision=high)  24.4 us
    dot_general x1, matrix products, form_beams(): jnp.einsum('pxf,bxf->bpf', sin_weight, windows_imag, precision=high)  23.7 us
    dot_general x1, matrix products, form_beams(): jnp.einsum('pxf,bxf->bpf', sin_weight, windows_real, precision=high)  23.6 us
    dot_general x1, matrix products, shards(): jnp.dot(traces[0].astype(jnp.float32), dft_table, precision=high)  19.2 us
  transfers between devices with their start and end apart: 18, of which 6 were waited for; matrix products, arithmetic and copies ran while one was open for 2% of the time, Pallas kernels for 0%

profile of v1, /device:TPU:0, one launch (start us, length us, event | category | flops | bytes accessed | tf_op | source)
XLA Modules:
  0.0 310.0 jit_solution(11967952198505189087)
XLA Ops:
  6.6 0.9 copy-done
  7.4 19.2 %fusion.60 = f32[64,1024]{1,0:T(8,128)S(1)} fusion(s32[1024]{0:T(1024)S(1)} %fusion.69, pred[1024]{0:T(1024)(128)(4,1)S(1)} %fusion.66, bf16[1,64,1024]{2,1,0:T(8,128)(2,1)S(1)} %copy-done), kind=kOutput, calls=%fused_computation.60 | convolution fusion | flops 823132160 | bytes 398336 | tf_op jit(solution)/shard_map/dot_general | solution.py:103
  26.7 2.4 collective-permute-start
  29.1 1.5 collective-permute-start.1
  34.4 2.5 gather_fusion.1
  36.8 1.7 reshape.393
  38.5 2.0 fusion.83
  40.5 3.7 %copy.25 = f32[16,33,512]{1,0,2:T(8,128)} copy(f32[16,33,512]{2,1,0:T(8,128)S(1)} %get-tuple-element.148) | data formatting | bytes 2162688
  44.2 3.8 %copy.26 = f32[16,33,512]{1,0,2:T(8,128)} copy(f32[16,33,512]{2,1,0:T(8,128)S(1)} %get-tuple-element.149) | data formatting | bytes 2162688
  48.0 24.9 %fusion.16 = f32[512,16,16]{2,1,0:T(8,128)S(1)} fusion(f32[16,33,512]{1,0,2:T(8,128)} %copy.25, f32[512]{0:T(512)S(1)} %iota_convert_fusion, f32[16,33]{1,0:T(8,128)S(1)} %broadcast_multiply_fusion, f32[33]{0:T(128)S(1)} %broadcast_divide_fusion), kind=kOutput, calls=%fused_computation.23 | convolution fusion | flops 52445184 | bytes 1609924 | tf_op jit(solution)/shard_map/pxf,bxf->bpf/dot_general | solution.py:72
  72.9 24.4 %fusion.14 = f32[512,16,16]{2,1,0:T(8,128)} fusion(f32[16,33,512]{1,0,2:T(8,128)S(1)} %copy-done.2, f32[512]{0:T(512)S(1)} %iota_convert_fusion, f32[16,33]{1,0:T(8,128)S(1)} %broadcast_multiply_fusion, f32[33]{0:T(128)S(1)} %broadcast_divide_fusion), kind=kOutput, calls=%fused_computation.22 | convolution fusion | flops 52445184 | bytes 1609924 | tf_op jit(solution)/shard_map/pxf,bxf->bpf/dot_general | solution.py:75
  97.3 23.7 %add_bitcast_fusion = bf16[16,16,1,512]{1,0,3,2:T(8,128)(2,1)S(1)} fusion(f32[512,16,16]{2,1,0:T(8,128)S(1)} %fusion.16, f32[16,33,512]{1,0,2:T(8,128)S(1)} %copy-done.2, f32[512]{0:T(512)S(1)} %iota_convert_fusion, f32[16,33]{1,0:T(8,128)S(1)} %broadcast_multiply_fusion, f32[33]{0:T(128)S(1)} %broadcast_divide_fusion), kind=kOutput, calls=%fused_computation.31 | convolution fusion | flops 52707328 | bytes 1872068 | tf_op jit(solution)/shard_map/pxf,bxf->bpf/dot_general | solution.py:72
  121.0 1.6 copy.22
  122.6 23.6 %subtract_bitcast_fusion = bf16[16,16,1,512]{1,0,3,2:T(8,128)(2,1)S(1)} fusion(f32[512,16,16]{2,1,0:T(8,128)} %fusion.14, f32[16,33,512]{1,0,2:T(8,128)} %copy.25, f32[512]{0:T(512)S(1)} %iota_convert_fusion, f32[16,33]{1,0:T(8,128)S(1)} %broadcast_multiply_fusion, f32[33]{0:T(128)S(1)} %broadcast_divide_fusion), kind=kOutput, calls=%fused_computation.30 | convolution fusion | flops 52707328 | bytes 1872068 | tf_op jit(solution)/shard_map/pxf,bxf->bpf/dot_general | solution.py:75
  146.2 1.8 copy.23
  148.6 1.1 fusion.84
  149.7 5.9 %collective-permute-start.2 = (bf16[16,1,1,1024]{3,0,2,1:T(8,128)(2,1)S(1)}, bf16[16,1,1,1024]{3,0,2,1:T(8,128)(2,1)S(1)}, u32[]{:S(2)}, u32[]{:S(2)}) collective-permute-start(bf16[16,1,1,1024]{3,0,2,1:T(8,128)(2,1)S(1)} %copy.28), channel_id=1, source_target_pairs={{0,30},{2,0},{4,2},{6,4},{8,6},{10,8},{12,10},{14,12},{16,14},{18,... | collective-permute-start | bytes 98312 | tf_op jit(solution)/shard_map/ppermute | solution.py:22
  156.4 1.3 gather_fusion
  157.6 1.8 collective-permute-start.3
  161.1 5.0 %collective-permute-start.7 = (bf16[16,1,1,1024]{3,0,2,1:T(8,128)(2,1)S(1)}, bf16[16,1,1,1024]{3,0,2,1:T(8,128)(2,1)S(1)}, u32[]{:S(2)}, u32[]{:S(2)}) collective-permute-start(bf16[16,1,1,1024]{3,0,2,1:T(8,128)(2,1)S(1)} %copy.33), channel_id=1, source_target_pairs={{0,20},{2,22},{4,24},{6,26},{8,28},{10,30},{12,0},{14,2},{16,4},{1... | collective-permute-start | bytes 98312 | tf_op jit(solution)/shard_map/ppermute | solution.py:22
  166.9 1.9 collective-permute-start.10
  168.8 2.0 collective-permute-start.11
  171.1 1.9 collective-permute-start.13
  173.0 2.1 collective-permute-start.14
  175.1 1.5 collective-permute-start.15
  176.8 1.9 collective-permute-done.14
  178.6 3.1 collective-permute-done.15
  181.7 0.9 collective-permute-done.16
  182.9 0.9 gather_fusion.2
  183.8 56.2 %while.14 = (s32[]{:T(128)}, f32[256,256]{1,0:T(8,128)S(1)}, s32[128,1]{0,1:T(1,128)S(1)}, bf16[128,1,1024]{2,0,1:T(8,128)(2,1)S(1)}, bf16[1024,1,4096]{2,0,1:T(...) while((s32[]{:T(128)}, f32[256,256]{1,0:T(8,128)S(1)}, ...), condition=%wide.region_6.7_spmd.clone, body=%wide.region_4.6_spmd.clone.sunk | while | flops 134349840 | bytes 10000863 | solution.py:155
  183.8 4.6 %fusion.95 = f32[16,1,4096]{2,0,1:T(8,128)S(1)} fusion(bf16[1024,1,4096]{2,0,1:T(8,128)(2,1)} %get-tuple-element.229, bf16[128,1,1024]{2,0,1:T(8,128)(2,1)S(1)} %get-tuple-element.228, s32[]{:T(128)S(6)} %select_n.239), kind=kOutput, calls=%fused_computation.8.clone.1 | convolution fusion | flops 134283264 | bytes 8683524 | tf_op jit(solution)/shard_map/while/body/eval_jaxpr/rsk,ksc->rsc/dot_general | solution.py:143
  188.7 2.1 scatter_fusion
  190.8 4.6 %fusion.95 = f32[16,1,4096]{2,0,1:T(8,128)S(1)} fusion(bf16[1024,1,4096]{2,0,1:T(8,128)(2,1)} %get-tuple-element.229, bf16[128,1,1024]{2,0,1:T(8,128)(2,1)S(1)} %get-tuple-element.228, s32[]{:T(128)S(6)} %select_n.239), kind=kOutput, calls=%fused_computation.8.clone.1 | convolution fusion | flops 134283264 | bytes 8683524 | tf_op jit(solution)/shard_map/while/body/eval_jaxpr/rsk,ksc->rsc/dot_general | solution.py:143
  195.7 2.1 scatter_fusion
  197.8 4.6 %fusion.95 = f32[16,1,4096]{2,0,1:T(8,128)S(1)} fusion(bf16[1024,1,4096]{2,0,1:T(8,128)(2,1)} %get-tuple-element.229, bf16[128,1,1024]{2,0,1:T(8,128)(2,1)S(1)} %get-tuple-element.228, s32[]{:T(128)S(6)} %select_n.239), kind=kOutput, calls=%fused_computation.8.clone.1 | convolution fusion | flops 134283264 | bytes 8683524 | tf_op jit(solution)/shard_map/while/body/eval_jaxpr/rsk,ksc->rsc/dot_general | solution.py:143
  202.8 2.1 scatter_fusion
  204.9 4.6 %fusion.95 = f32[16,1,4096]{2,0,1:T(8,128)S(1)} fusion(bf16[1024,1,4096]{2,0,1:T(8,128)(2,1)} %get-tuple-element.229, bf16[128,1,1024]{2,0,1:T(8,128)(2,1)S(1)} %get-tuple-element.228, s32[]{:T(128)S(6)} %select_n.239), kind=kOutput, calls=%fused_computation.8.clone.1 | convolution fusion | flops 134283264 | bytes 8683524 | tf_op jit(solution)/shard_map/while/body/eval_jaxpr/rsk,ksc->rsc/dot_general | solution.py:143
  209.8 2.1 scatter_fusion
  211.9 4.6 %fusion.95 = f32[16,1,4096]{2,0,1:T(8,128)S(1)} fusion(bf16[1024,1,4096]{2,0,1:T(8,128)(2,1)} %get-tuple-element.229, bf16[128,1,1024]{2,0,1:T(8,128)(2,1)S(1)} %get-tuple-element.228, s32[]{:T(128)S(6)} %select_n.239), kind=kOutput, calls=%fused_computation.8.clone.1 | convolution fusion | flops 134283264 | bytes 8683524 | tf_op jit(solution)/shard_map/while/body/eval_jaxpr/rsk,ksc->rsc/dot_general | solution.py:143
  216.8 2.1 scatter_fusion
  218.9 4.6 %fusion.95 = f32[16,1,4096]{2,0,1:T(8,128)S(1)} fusion(bf16[1024,1,4096]{2,0,1:T(8,128)(2,1)} %get-tuple-element.229, bf16[128,1,1024]{2,0,1:T(8,128)(2,1)S(1)} %get-tuple-element.228, s32[]{:T(128)S(6)} %select_n.239), kind=kOutput, calls=%fused_computation.8.clone.1 | convolution fusion | flops 134283264 | bytes 8683524 | tf_op jit(solution)/shard_map/while/body/eval_jaxpr/rsk,ksc->rsc/dot_general | solution.py:143
  223.8 2.1 scatter_fusion
  225.9 4.6 %fusion.95 = f32[16,1,4096]{2,0,1:T(8,128)S(1)} fusion(bf16[1024,1,4096]{2,0,1:T(8,128)(2,1)} %get-tuple-element.229, bf16[128,1,1024]{2,0,1:T(8,128)(2,1)S(1)} %get-tuple-element.228, s32[]{:T(128)S(6)} %select_n.239), kind=kOutput, calls=%fused_computation.8.clone.1 | convolution fusion | flops 134283264 | bytes 8683524 | tf_op jit(solution)/shard_map/while/body/eval_jaxpr/rsk,ksc->rsc/dot_general | solution.py:143
  230.8 2.1 scatter_fusion
  232.9 4.6 %fusion.95 = f32[16,1,4096]{2,0,1:T(8,128)S(1)} fusion(bf16[1024,1,4096]{2,0,1:T(8,128)(2,1)} %get-tuple-element.229, bf16[128,1,1024]{2,0,1:T(8,128)(2,1)S(1)} %get-tuple-element.228, s32[]{:T(128)S(6)} %select_n.239), kind=kOutput, calls=%fused_computation.8.clone.1 | convolution fusion | flops 134283264 | bytes 8683524 | tf_op jit(solution)/shard_map/while/body/eval_jaxpr/rsk,ksc->rsc/dot_general | solution.py:143
  237.9 2.1 scatter_fusion
  240.7 53.1 %reduce-scatter.2.cloned.1.call-done = f32[16,256]{1,0:T(8,128)} async-done(((f32[256,256]{1,0:T(8,128)}), f32[16,256]{1,0:T(8,128)}) %reduce-scatter.2.cloned.1.call-update) | async-done | bytes 16400 | tf_op jit(solution)/shard_map/reduce_scatter | solution.py:156
  293.8 9.4 %psum.7 = f32[16,256]{1,0:T(8,128)} all-reduce(f32[16,256]{1,0:T(8,128)} %reduce-scatter.2.cloned.1.call-done), channel_id=1, replica_groups=mesh['grp'=1,'mid'=16,'off'=2,'sub'=1] {'off','sub'}, use_global_device_ids=true, to_apply=%region_8.9 | all-reduce | flops 4096 | bytes 32768 | tf_op jit(solution)/shard_map/psum | solution.py:157
  (155 shorter events, 10.5 us)
Async XLA Ops:
  6.5 0.9 copy-start
  6.5 287.3 %reduce-scatter.2.cloned.1.call-start = ((), (), s32[]{:S(2)}) async-start(), calls=%async_computation.1 | async-start | bytes 278528 | tf_op jit(solution)/shard_map/reduce_scatter | solution.py:156
  7.4 23.8 %copy-start.4 = (s32[16]{0:T(128)S(1)}, s32[16]{0:T(128)}, u32[]{:S(2)}) copy-start(s32[16]{0:T(128)} %param.10) | copy-start | bytes 196
  7.4 24.2 %copy-start.3 = (s32[16]{0:T(128)S(1)}, s32[16]{0:T(128)}, u32[]{:S(2)}) copy-start(s32[16]{0:T(128)} %param.8) | copy-start | bytes 196
  26.7 7.2 %collective-permute-start = (f32[16,1024]{1,0:T(8,128)S(1)}, f32[16,1024]{1,0:T(8,128)S(1)}, u32[]{:S(2)}, u32[]{:S(2)}) collective-permute-start(f32[16,1024]{1,0:T(8,128)S(1)} %get-tuple-element.166), channel_id=1, source_target_pairs={{0,2},{2,4},{4,6},{6,8},{8,10},{10,12},{12,14},{14,16},{16,18},{18... | collective-permute-start | bytes 196616 | tf_op jit(solution)/shard_map/ppermute | solution.py:35
  29.1 5.3 %collective-permute-start.1 = (f32[16,1024]{1,0:T(8,128)S(1)}, f32[16,1024]{1,0:T(8,128)S(1)}, u32[]{:S(2)}, u32[]{:S(2)}) collective-permute-start(f32[16,1024]{1,0:T(8,128)S(1)} %get-tuple-element.167), channel_id=1, source_target_pairs={{2,0},{4,2},{6,4},{8,6},{10,8},{12,10},{14,12},{16,14},{18,16},{20... | collective-permute-start | bytes 196616 | tf_op jit(solution)/shard_map/ppermute | solution.py:37
  48.0 24.9 %copy-start.2 = (f32[16,33,512]{1,0,2:T(8,128)S(1)}, f32[16,33,512]{1,0,2:T(8,128)}, u32[]{:S(2)}) copy-start(f32[16,33,512]{1,0,2:T(8,128)} %copy.26) | copy-start | bytes 3244036
  149.7 11.3 %collective-permute-start.2 = (bf16[16,1,1,1024]{3,0,2,1:T(8,128)(2,1)S(1)}, bf16[16,1,1,1024]{3,0,2,1:T(8,128)(2,1)S(1)}, u32[]{:S(2)}, u32[]{:S(2)}) collective-permute-start(bf16[16,1,1,1024]{3,0,2,1:T(8,128)(2,1)S(1)} %copy.28), channel_id=1, source_target_pairs={{0,30},{2,0},{4,2},{6,4},{8,6},{10,8},{12,10},{14,12},{16,14},{18,... | collective-permute-start | bytes 98312 | tf_op jit(solution)/shard_map/ppermute | solution.py:22
  157.6 8.4 %collective-permute-start.3 = (bf16[16,1,1,1024]{3,0,2,1:T(8,128)(2,1)S(1)}, bf16[16,1,1,1024]{3,0,2,1:T(8,128)(2,1)S(1)}, u32[]{:S(2)}, u32[]{:S(2)}) collective-permute-start(bf16[16,1,1,1024]{3,0,2,1:T(8,128)(2,1)S(1)} %copy.29), channel_id=1, source_target_pairs={{0,28},{2,30},{4,0},{6,2},{8,4},{10,6},{12,8},{14,10},{16,12},{18,... | collective-permute-start | bytes 98312 | tf_op jit(solution)/shard_map/ppermute | solution.py:22
  159.4 6.6 %collective-permute-start.4 = (bf16[16,1,1,1024]{3,0,2,1:T(8,128)(2,1)S(1)}, bf16[16,1,1,1024]{3,0,2,1:T(8,128)(2,1)S(1)}, u32[]{:S(2)}, u32[]{:S(2)}) collective-permute-start(bf16[16,1,1,1024]{3,0,2,1:T(8,128)(2,1)S(1)} %copy.30), channel_id=1, source_target_pairs={{0,26},{2,28},{4,30},{6,0},{8,2},{10,4},{12,6},{14,8},{16,10},{18,... | collective-permute-start | bytes 98312 | tf_op jit(solution)/shard_map/ppermute | solution.py:22
  160.1 6.8 %collective-permute-start.5 = (bf16[16,1,1,1024]{3,0,2,1:T(8,128)(2,1)S(1)}, bf16[16,1,1,1024]{3,0,2,1:T(8,128)(2,1)S(1)}, u32[]{:S(2)}, u32[]{:S(2)}) collective-permute-start(bf16[16,1,1,1024]{3,0,2,1:T(8,128)(2,1)S(1)} %copy.31), channel_id=1, source_target_pairs={{0,24},{2,26},{4,28},{6,30},{8,0},{10,2},{12,4},{14,6},{16,8},{18,... | collective-permute-start | bytes 98312 | tf_op jit(solution)/shard_map/ppermute | solution.py:22
  160.6 8.2 %collective-permute-start.6 = (bf16[16,1,1,1024]{3,0,2,1:T(8,128)(2,1)S(1)}, bf16[16,1,1,1024]{3,0,2,1:T(8,128)(2,1)S(1)}, u32[]{:S(2)}, u32[]{:S(2)}) collective-permute-start(bf16[16,1,1,1024]{3,0,2,1:T(8,128)(2,1)S(1)} %copy.32), channel_id=1, source_target_pairs={{0,22},{2,24},{4,26},{6,28},{8,30},{10,0},{12,2},{14,4},{16,6},{18... | collective-permute-start | bytes 98312 | tf_op jit(solution)/shard_map/ppermute | solution.py:22
  161.1 9.8 %collective-permute-start.7 = (bf16[16,1,1,1024]{3,0,2,1:T(8,128)(2,1)S(1)}, bf16[16,1,1,1024]{3,0,2,1:T(8,128)(2,1)S(1)}, u32[]{:S(2)}, u32[]{:S(2)}) collective-permute-start(bf16[16,1,1,1024]{3,0,2,1:T(8,128)(2,1)S(1)} %copy.33), channel_id=1, source_target_pairs={{0,20},{2,22},{4,24},{6,26},{8,28},{10,30},{12,0},{14,2},{16,4},{1... | collective-permute-start | bytes 98312 | tf_op jit(solution)/shard_map/ppermute | solution.py:22
  166.0 5.0 %collective-permute-start.8 = (bf16[16,1,1,1024]{3,0,2,1:T(8,128)(2,1)S(1)}, bf16[16,1,1,1024]{3,0,2,1:T(8,128)(2,1)S(1)}, u32[]{:S(2)}, u32[]{:S(2)}) collective-permute-start(bf16[16,1,1,1024]{3,0,2,1:T(8,128)(2,1)S(1)} %copy.34), channel_id=1, source_target_pairs={{0,18},{2,20},{4,22},{6,24},{8,26},{10,28},{12,30},{14,0},{16,2},{... | collective-permute-start | bytes 98312 | tf_op jit(solution)/shard_map/ppermute | solution.py:22
  166.1 6.9 %collective-permute-start.9 = (bf16[16,1,1,1024]{3,0,2,1:T(8,128)(2,1)S(1)}, bf16[16,1,1,1024]{3,0,2,1:T(8,128)(2,1)S(1)}, u32[]{:S(2)}, u32[]{:S(2)}) collective-permute-start(bf16[16,1,1,1024]{3,0,2,1:T(8,128)(2,1)S(1)} %copy.35), channel_id=1, source_target_pairs={{0,16},{2,18},{4,20},{6,22},{8,24},{10,26},{12,28},{14,30},{16,0},... | collective-permute-start | bytes 98312 | tf_op jit(solution)/shard_map/ppermute | solution.py:22
  166.9 8.2 %collective-permute-start.10 = (bf16[16,1,1,1024]{3,0,2,1:T(8,128)(2,1)S(1)}, bf16[16,1,1,1024]{3,0,2,1:T(8,128)(2,1)S(1)}, u32[]{:S(2)}, u32[]{:S(2)}) collective-permute-start(bf16[16,1,1,1024]{3,0,2,1:T(8,128)(2,1)S(1)} %copy.36), channel_id=1, source_target_pairs={{0,14},{2,16},{4,18},{6,20},{8,22},{10,24},{12,26},{14,28},{16,30}... | collective-permute-start | bytes 98312 | tf_op jit(solution)/shard_map/ppermute | solution.py:22
  168.8 7.8 %collective-permute-start.11 = (bf16[16,1,1,1024]{3,0,2,1:T(8,128)(2,1)S(1)}, bf16[16,1,1,1024]{3,0,2,1:T(8,128)(2,1)S(1)}, u32[]{:S(2)}, u32[]{:S(2)}) collective-permute-start(bf16[16,1,1,1024]{3,0,2,1:T(8,128)(2,1)S(1)} %copy.37), channel_id=1, source_target_pairs={{0,12},{2,14},{4,16},{6,18},{8,20},{10,22},{12,24},{14,26},{16,28}... | collective-permute-start | bytes 98312 | tf_op jit(solution)/shard_map/ppermute | solution.py:22
  170.8 5.8 %collective-permute-start.12 = (bf16[16,1,1,1024]{3,0,2,1:T(8,128)(2,1)S(1)}, bf16[16,1,1,1024]{3,0,2,1:T(8,128)(2,1)S(1)}, u32[]{:S(2)}, u32[]{:S(2)}) collective-permute-start(bf16[16,1,1,1024]{3,0,2,1:T(8,128)(2,1)S(1)} %copy.38), channel_id=1, source_target_pairs={{0,10},{2,12},{4,14},{6,16},{8,18},{10,20},{12,22},{14,24},{16,26}... | collective-permute-start | bytes 98312 | tf_op jit(solution)/shard_map/ppermute | solution.py:22
  171.1 5.7 %collective-permute-start.13 = (bf16[16,1,1,1024]{3,0,2,1:T(8,128)(2,1)S(1)}, bf16[16,1,1,1024]{3,0,2,1:T(8,128)(2,1)S(1)}, u32[]{:S(2)}, u32[]{:S(2)}) collective-permute-start(bf16[16,1,1,1024]{3,0,2,1:T(8,128)(2,1)S(1)} %copy.39), channel_id=1, source_target_pairs={{0,8},{2,10},{4,12},{6,14},{8,16},{10,18},{12,20},{14,22},{16,24},... | collective-permute-start | bytes 98312 | tf_op jit(solution)/shard_map/ppermute | solution.py:22
  173.0 5.6 %collective-permute-start.14 = (bf16[16,1,1,1024]{3,0,2,1:T(8,128)(2,1)S(1)}, bf16[16,1,1,1024]{3,0,2,1:T(8,128)(2,1)S(1)}, u32[]{:S(2)}, u32[]{:S(2)}) collective-permute-start(bf16[16,1,1,1024]{3,0,2,1:T(8,128)(2,1)S(1)} %copy.40), channel_id=1, source_target_pairs={{0,6},{2,8},{4,10},{6,12},{8,14},{10,16},{12,18},{14,20},{16,22},{... | collective-permute-start | bytes 98312 | tf_op jit(solution)/shard_map/ppermute | solution.py:22
  175.1 6.6 %collective-permute-start.15 = (bf16[16,1,1,1024]{3,0,2,1:T(8,128)(2,1)S(1)}, bf16[16,1,1,1024]{3,0,2,1:T(8,128)(2,1)S(1)}, u32[]{:S(2)}, u32[]{:S(2)}) collective-permute-start(bf16[16,1,1,1024]{3,0,2,1:T(8,128)(2,1)S(1)} %copy.41), channel_id=1, source_target_pairs={{0,4},{2,6},{4,8},{6,10},{8,12},{10,14},{12,16},{14,18},{16,20},{1... | collective-permute-start | bytes 98312 | tf_op jit(solution)/shard_map/ppermute | solution.py:22
  176.6 6.0 %collective-permute-start.16 = (bf16[16,1,1,1024]{3,0,2,1:T(8,128)(2,1)S(1)}, bf16[16,1,1,1024]{3,0,2,1:T(8,128)(2,1)S(1)}, u32[]{:S(2)}, u32[]{:S(2)}) collective-permute-start(bf16[16,1,1,1024]{3,0,2,1:T(8,128)(2,1)S(1)} %copy.42), channel_id=1, source_target_pairs={{0,2},{2,4},{4,6},{6,8},{8,10},{10,12},{12,14},{14,16},{16,18},{18... | collective-permute-start | bytes 98312 | tf_op jit(solution)/shard_map/ppermute | solution.py:22
  239.9 0.7 copy-start.1
Sparse Core Ops, SparseCore 0:
  240.8 52.9 reduce-scatter.1
